TPU v7x, 256 devices: a whole 4x4x8 slice. The times are simulated.
256 devices in a mesh: zero: 32 (over z_0, y, x), width: 2 (over z_1), site: 4 (over z_2, core).
Axes of the slice: x: 4, y: 4, z: 8 (z_0: 2, z_1: 2, z_2: 2; z = z_0 * 4 + z_1 * 2 + z_2), core: 2. Of those that a mesh axis runs over, the one named last changes fastest.
Arguments:
- train_query: bfloat16 [28672, 7168], P(('site', 'zero'), 'width'), parts along dimension 0, may hold values from -0.125 to 0.125
- low_query: bfloat16 [28672, 64], P(('site', 'zero')), parts along dimension 0, may hold values from -0.0625 to 0.0625
- high_query: bfloat16 [256, 7168], P('site', 'width'), parts along dimension 0, may hold values from -0.75 to 0.75
- train_key: bfloat16 [28672, 7168], P(('site', 'zero'), 'width'), parts along dimension 0, may hold values from -0.125 to 0.125
- low_key: bfloat16 [28672, 64], P(('site', 'zero')), parts along dimension 0, may hold values from -0.0625 to 0.0625
- high_key: bfloat16 [256, 7168], P('site', 'width'), parts along dimension 0, may hold values from -0.75 to 0.75
- train_value: bfloat16 [28672, 7168], P(('site', 'zero'), 'width'), parts along dimension 0, may hold values from -0.125 to 0.125
- low_value: bfloat16 [28672, 64], P(('site', 'zero')), parts along dimension 0, may hold values from -0.0625 to 0.0625
- high_value: bfloat16 [256, 7168], P('site', 'width'), parts along dimension 0, may hold values from -0.75 to 0.75
- norm_train: float32 [28672], P(('site', 'zero', 'width')), parts along dimension 0, may hold values from 0.25 to 1.75
- norm_step: float32 [28672], P(('site', 'zero', 'width')), parts along dimension 0, may hold values from -0.3 to 0.3
Outputs:
- final_query: bfloat16 [28672, 7168], P('site', ('width', 'zero')), parts along dimension 0
- final_key: bfloat16 [28672, 7168], P('site', ('width', 'zero')), parts along dimension 0
- final_value: bfloat16 [28672, 7168], P('site', ('width', 'zero')), parts along dimension 0
- scale_query: float32 [28672], P(('site', 'width', 'zero')), parts along dimension 0
- scale_key: float32 [28672], P(('site', 'width', 'zero')), parts along dimension 0
- scale_value: float32 [28672], P(('site', 'width', 'zero')), parts along dimension 0
- serve_norm: bfloat16 [28672], P('site'), parts along dimension 0
There are 4 independent parts, one for each index of `site`. A program takes and returns all parts, laid end to end along the dimension named above; each array names one. Nothing has to cross between parts.
All inputs are finite; a program needn't handle non-finite values. Where the computation divides by a largest or mean magnitude, that divisor is 1e-20 or more.
Results may differ from a plain program's by a relative error of at most 0.01.
Values may be sent and summed in bfloat16 or wider, within the bound.
A program may use at most 128 MiB of HBM per device.

v0:
```python
import jax
import jax.numpy as jnp
from jax import lax
from jax.sharding import PartitionSpec as P

D_MODEL = 7168


mix_rate = 1.0


def copy_for_each(array, axis):
    peers = lax.axis_size(axis)
    return lax.all_to_all(
        jnp.broadcast_to(array[None], (peers, *array.shape)), axis, 0, 0, tiled=True
    )


def taken_together(array, axis):
    everything = copy_for_each(array, axis)
    return jnp.sum(everything.astype(jnp.float32), axis=0)


def in_order(blocks, dim):
    blocks = jnp.moveaxis(blocks, 0, dim)
    shape = blocks.shape
    return blocks.reshape(*shape[:dim], shape[dim] * shape[dim + 1], *shape[dim + 2 :])


def collect(array, axis, dim):
    return in_order(copy_for_each(array, axis), dim)


def shards(
    train_query,
    low_query,
    high_query,
    train_key,
    low_key,
    high_key,
    train_value,
    low_value,
    high_value,
    norm_train,
    norm_step,
):
    result_query = train_query.astype(jnp.float32) + mix_rate * jnp.dot(
        low_query, high_query, preferred_element_type=jnp.float32
    )
    result_key = train_key.astype(jnp.float32) + mix_rate * jnp.dot(
        low_key, high_key, preferred_element_type=jnp.float32
    )
    result_value = train_value.astype(jnp.float32) + mix_rate * jnp.dot(
        low_value, high_value, preferred_element_type=jnp.float32
    )
    total_query, total_key, total_value = (
        taken_together(jnp.sum(jnp.abs(result_query), axis=0).astype(jnp.bfloat16), "zero").astype(
            jnp.float32
        ),
        taken_together(jnp.sum(jnp.abs(result_key), axis=0).astype(jnp.bfloat16), "zero").astype(
            jnp.float32
        ),
        taken_together(jnp.sum(jnp.abs(result_value), axis=0).astype(jnp.bfloat16), "zero").astype(
            jnp.float32
        ),
    )
    scale_query = total_query / D_MODEL
    scale_key = total_key / D_MODEL
    scale_value = total_value / D_MODEL
    narrow_query, narrow_key, narrow_value = (
        (result_query / scale_query).astype(jnp.bfloat16),
        (result_key / scale_key).astype(jnp.bfloat16),
        (result_value / scale_value).astype(jnp.bfloat16),
    )
    final_query, final_key, final_value = (
        lax.all_to_all(narrow_query, "zero", split_axis=1, concat_axis=0, tiled=True),
        lax.all_to_all(narrow_key, "zero", split_axis=1, concat_axis=0, tiled=True),
        lax.all_to_all(narrow_value, "zero", split_axis=1, concat_axis=0, tiled=True),
    )
    place = lax.axis_index("zero")
    scale_query = lax.dynamic_slice_in_dim(
        scale_query, place * final_query.shape[1], final_query.shape[1]
    )
    scale_key = lax.dynamic_slice_in_dim(scale_key, place * final_key.shape[1], final_key.shape[1])
    scale_value = lax.dynamic_slice_in_dim(
        scale_value, place * final_value.shape[1], final_value.shape[1]
    )
    serve_norm = collect((norm_train + norm_step).astype(jnp.bfloat16), ("zero", "width"), 0)
    return (final_query, final_key, final_value, scale_query, scale_key, scale_value, serve_norm)


def solution(mesh):
    in_specs = (
        P(("site", "zero"), "width"),
        P(("site", "zero"), None),
        P("site", "width"),
        P(("site", "zero"), "width"),
        P(("site", "zero"), None),
        P("site", "width"),
        P(("site", "zero"), "width"),
        P(("site", "zero"), None),
        P("site", "width"),
        P(("site", "zero", "width")),
        P(("site", "zero", "width")),
    )
    out_specs = (
        P("site", ("width", "zero")),
        P("site", ("width", "zero")),
        P("site", ("width", "zero")),
        P(("site", "width", "zero")),
        P(("site", "width", "zero")),
        P(("site", "width", "zero")),
        P("site"),
    )
    return jax.shard_map(shards, mesh=mesh, in_specs=in_specs, out_specs=out_specs, check_vma=False)
```

profile of v0, /device:TPU:64, one launch (start us, length us, event | category | flops | bytes accessed | tf_op | source)
XLA Modules:
  0.0 234.4 jit_solution(13846646193369663413)
XLA Ops:
  0.6 0.7 add_convert_fusion
  1.4 0.6 broadcast_in_dim.11
  2.0 13.8 %all-to-all-start.6 = ((bf16[64,1,112]{2,1,0:T(2,128)(2,1)}), bf16[64,1,112]{2,1,0:T(2,128)(2,1)S(1)}, u32[]{:S(2)}, u32[]{:S(2)}) async-start(bf16[64,1,112]{2,1,0:T(2,128)(2,1)} %broadcast_in_dim.11), calls=%async_computation.6 | async-start | bytes 65536 | tf_op jit(solution)/shard_map/all_to_all | solution.py:14
  15.8 4.0 %abs_reduce_fusion.2 = (bf16[3584]{0:T(1024)(128)(2,1)S(1)}, f32[224,3584]{1,0:T(8,128)}) fusion(bf16[224,64]{0,1:T(8,128)(2,1)} %param.12, bf16[64,3584]{1,0:T(8,128)(2,1)S(1)} %copy-done, bf16[224,3584]{1,0:T(8,128)(2,1)} %param.11), kind=kOutput, calls=%fused_computation.8 | convolution fusion | flops 105968128 | bytes 5311488 | tf_op jit(solution)/shard_map/dot_general | solution.py:47
  19.8 0.2 broadcast_in_dim.8
  20.0 0.5 broadcast.41
  20.6 2.0 reduce.4
  22.5 0.7 reshape.74
  23.3 2.5 %all-to-all-done.6 = bf16[64,1,112]{2,1,0:T(2,128)(2,1)S(1)} async-done(((bf16[64,1,112]{2,1,0:T(2,128)(2,1)}), bf16[64,1,112]{2,1,0:T(2,128)(2,1)S(1)}, u32[]{:S(2)}, u32[]{:S(2)}) %all-to-all-start.6) | async-done | bytes 14368 | tf_op jit(solution)/shard_map/all_to_all | solution.py:14
  25.8 7.8 %all-to-all-start = ((bf16[32,2,1792]{2,1,0:T(2,128)(2,1)}), bf16[32,2,1792]{2,1,0:T(2,128)(2,1)S(1)}, u32[]{:S(2)}, u32[]{:S(2)}) async-start(bf16[32,2,1792]{2,1,0:T(2,128)(2,1)} %reshape.74), calls=%async_computation | async-start | bytes 458752 | tf_op jit(solution)/shard_map/all_to_all | solution.py:14
  33.6 2.4 %abs_reduce_fusion.1 = (bf16[3584]{0:T(1024)(128)(2,1)S(1)}, f32[224,3584]{1,0:T(8,128)}) fusion(bf16[224,64]{0,1:T(8,128)(2,1)S(1)} %copy-done.3, bf16[64,3584]{1,0:T(8,128)(2,1)S(1)} %copy-done.2, bf16[224,3584]{1,0:T(8,128)(2,1)S(1)} %copy-done.1), kind=kOutput, calls=%fused_computation.6 | convolution fusion | flops 105968128 | bytes 5311488 | tf_op jit(solution)/shard_map/dot_general | solution.py:50
  36.0 0.2 broadcast_in_dim.9
  36.2 2.0 reduce.5
  38.2 0.7 reshape.76
  39.0 8.5 %all-to-all-done = bf16[32,2,1792]{2,1,0:T(2,128)(2,1)S(1)} async-done(((bf16[32,2,1792]{2,1,0:T(2,128)(2,1)}), bf16[32,2,1792]{2,1,0:T(2,128)(2,1)S(1)}, u32[]{:S(2)}, u32[]{:S(2)}) %all-to-all-start) | async-done | bytes 229408 | tf_op jit(solution)/shard_map/all_to_all | solution.py:14
  47.5 5.1 %all-to-all-start.2 = ((bf16[32,2,1792]{2,1,0:T(2,128)(2,1)}), bf16[32,2,1792]{2,1,0:T(2,128)(2,1)S(1)}, u32[]{:S(2)}, u32[]{:S(2)}) async-start(bf16[32,2,1792]{2,1,0:T(2,128)(2,1)} %reshape.76), calls=%async_computation.2 | async-start | bytes 458752 | tf_op jit(solution)/shard_map/all_to_all | solution.py:14
  52.6 3.9 %abs_reduce_fusion = (bf16[3584]{0:T(1024)(128)(2,1)S(1)}, f32[224,3584]{1,0:T(8,128)}) fusion(bf16[224,64]{0,1:T(8,128)(2,1)S(1)} %copy-done.4, bf16[64,3584]{1,0:T(8,128)(2,1)} %param.19, bf16[224,3584]{1,0:T(8,128)(2,1)} %param.17), kind=kOutput, calls=%fused_computation.4 | convolution fusion | flops 105968128 | bytes 5311488 | tf_op jit(solution)/shard_map/dot_general | solution.py:53
  56.5 0.2 broadcast_in_dim.10
  56.7 2.0 reduce.6
  58.7 0.7 reshape.78
  59.5 0.2 reshape.75
  59.7 6.4 %all-to-all-done.2 = bf16[32,2,1792]{2,1,0:T(2,128)(2,1)S(1)} async-done(((bf16[32,2,1792]{2,1,0:T(2,128)(2,1)}), bf16[32,2,1792]{2,1,0:T(2,128)(2,1)S(1)}, u32[]{:S(2)}, u32[]{:S(2)}) %all-to-all-start.2) | async-done | bytes 229408 | tf_op jit(solution)/shard_map/all_to_all | solution.py:14
  66.1 5.8 %all-to-all-start.4 = ((bf16[32,2,1792]{2,1,0:T(2,128)(2,1)}), bf16[32,2,1792]{2,1,0:T(2,128)(2,1)S(1)}, u32[]{:S(2)}, u32[]{:S(2)}) async-start(bf16[32,2,1792]{2,1,0:T(2,128)(2,1)} %reshape.78), calls=%async_computation.4 | async-start | bytes 458752 | tf_op jit(solution)/shard_map/all_to_all | solution.py:14
  72.0 3.3 %divide_convert_fusion.2 = bf16[224,3584]{1,0:T(8,128)(2,1)} fusion(f32[224,3584]{1,0:T(8,128)} %get-tuple-element.36, f32[3584]{0:T(1024)S(1)} %broadcast_multiply_fusion.2), kind=kLoop, calls=%fused_computation.7 | loop fusion | flops 1605632 | bytes 4831232 | tf_op jit(solution)/shard_map/convert_element_type | solution.py:71
  75.2 3.8 %all_to_all.59 = bf16[224,32,112]{2,1,0:T(8,128)(2,1)S(1)} reshape(bf16[224,3584]{1,0:T(8,128)(2,1)} %divide_convert_fusion.2) | data formatting | bytes 3211264 | tf_op jit(solution)/shard_map/all_to_all | solution.py:76
  79.1 2.0 copy.46
  81.0 3.9 %all-to-all-done.4 = bf16[32,2,1792]{2,1,0:T(2,128)(2,1)S(1)} async-done(((bf16[32,2,1792]{2,1,0:T(2,128)(2,1)}), bf16[32,2,1792]{2,1,0:T(2,128)(2,1)S(1)}, u32[]{:S(2)}, u32[]{:S(2)}) %all-to-all-start.4) | async-done | bytes 229408 | tf_op jit(solution)/shard_map/all_to_all | solution.py:14
  84.9 8.6 %all-to-all-start.1 = ((bf16[224,32,112]{2,0,1:T(8,128)(2,1)}), bf16[224,32,112]{2,0,1:T(8,128)(2,1)S(1)}, u32[]{:S(2)}, u32[]{:S(2)}) async-start(bf16[224,32,112]{2,0,1:T(8,128)(2,1)} %copy.46), calls=%async_computation.1 | async-start | bytes 3670016 | tf_op jit(solution)/shard_map/all_to_all | solution.py:76
  93.5 0.2 reshape.77
  93.7 3.3 %divide_convert_fusion.1 = bf16[224,3584]{1,0:T(8,128)(2,1)} fusion(f32[224,3584]{1,0:T(8,128)} %get-tuple-element.38, f32[3584]{0:T(1024)S(1)} %broadcast_multiply_fusion.1), kind=kLoop, calls=%fused_computation.5 | loop fusion | flops 1605632 | bytes 4831232 | tf_op jit(solution)/shard_map/convert_element_type | solution.py:72
  97.0 4.7 %all_to_all.64 = bf16[224,32,112]{2,1,0:T(8,128)(2,1)} reshape(bf16[224,3584]{1,0:T(8,128)(2,1)} %divide_convert_fusion.1) | data formatting | bytes 3211264 | tf_op jit(solution)/shard_map/all_to_all | solution.py:77
  101.7 3.5 %copy.48 = bf16[224,32,112]{2,0,1:T(8,128)(2,1)} copy(bf16[224,32,112]{2,1,0:T(8,128)(2,1)} %all_to_all.64) | data formatting | bytes 3211264 | tf_op jit(solution)/shard_map/all_to_all | solution.py:77
  105.2 32.5 %all-to-all-done.1 = bf16[224,32,112]{2,0,1:T(8,128)(2,1)S(1)} async-done(((bf16[224,32,112]{2,0,1:T(8,128)(2,1)}), bf16[224,32,112]{2,0,1:T(8,128)(2,1)S(1)}, u32[]{:S(2)}, u32[]{:S(2)}) %all-to-all-start.1) | async-done | bytes 1605664 | tf_op jit(solution)/shard_map/all_to_all | solution.py:76
  137.7 4.8 %all-to-all-start.3 = ((bf16[224,32,112]{2,0,1:T(8,128)(2,1)}), bf16[224,32,112]{2,0,1:T(8,128)(2,1)}, u32[]{:S(2)}, u32[]{:S(2)}) async-start(bf16[224,32,112]{2,0,1:T(8,128)(2,1)} %copy.48), calls=%async_computation.3 | async-start | bytes 3670016 | tf_op jit(solution)/shard_map/all_to_all | solution.py:77
  142.4 0.2 reshape.79
  142.7 3.3 %divide_convert_fusion = bf16[224,3584]{1,0:T(8,128)(2,1)} fusion(f32[224,3584]{1,0:T(8,128)} %get-tuple-element.40, f32[3584]{0:T(1024)S(1)} %broadcast_multiply_fusion), kind=kLoop, calls=%fused_computation.3 | loop fusion | flops 1605632 | bytes 4831232 | tf_op jit(solution)/shard_map/convert_element_type | solution.py:73
  146.0 4.8 %all_to_all.69 = bf16[224,32,112]{2,1,0:T(8,128)(2,1)} reshape(bf16[224,3584]{1,0:T(8,128)(2,1)} %divide_convert_fusion) | data formatting | bytes 3211264 | tf_op jit(solution)/shard_map/all_to_all | solution.py:78
  150.8 3.5 %copy.50 = bf16[224,32,112]{2,0,1:T(8,128)(2,1)} copy(bf16[224,32,112]{2,1,0:T(8,128)(2,1)} %all_to_all.69) | data formatting | bytes 3211264 | tf_op jit(solution)/shard_map/all_to_all | solution.py:78
  154.2 38.8 %all-to-all-done.3 = bf16[224,32,112]{2,0,1:T(8,128)(2,1)} async-done(((bf16[224,32,112]{2,0,1:T(8,128)(2,1)}), bf16[224,32,112]{2,0,1:T(8,128)(2,1)}, u32[]{:S(2)}, u32[]{:S(2)}) %all-to-all-start.3) | async-done | bytes 1605664 | tf_op jit(solution)/shard_map/all_to_all | solution.py:77
  193.1 10.8 %all-to-all-start.5 = ((bf16[224,32,112]{2,0,1:T(8,128)(2,1)}), bf16[224,32,112]{2,0,1:T(8,128)(2,1)}, u32[]{:S(2)}, u32[]{:S(2)}) async-start(bf16[224,32,112]{2,0,1:T(8,128)(2,1)} %copy.50), calls=%async_computation.5 | async-start | bytes 3670016 | tf_op jit(solution)/shard_map/all_to_all | solution.py:78
  204.0 0.7 reshape.72
  204.7 0.6 dynamic_slice.9
  205.3 0.6 dynamic_slice.10
  205.9 0.6 dynamic_slice.11
  206.4 2.8 %copy.51 = bf16[7168,112]{0,1:T(8,128)(2,1)} copy(bf16[7168,112]{1,0:T(8,128)(2,1)S(1)} %bitcast.15) | data formatting | bytes 3211264
  209.2 3.8 %copy.52 = bf16[7168,112]{0,1:T(8,128)(2,1)} copy(bf16[7168,112]{1,0:T(8,128)(2,1)} %bitcast.3) | data formatting | bytes 3211264
  213.1 17.5 %all-to-all-done.5 = bf16[224,32,112]{2,0,1:T(8,128)(2,1)} async-done(((bf16[224,32,112]{2,0,1:T(8,128)(2,1)}), bf16[224,32,112]{2,0,1:T(8,128)(2,1)}, u32[]{:S(2)}, u32[]{:S(2)}) %all-to-all-start.5) | async-done | bytes 1605664 | tf_op jit(solution)/shard_map/all_to_all | solution.py:78
  230.6 3.8 %copy.53 = bf16[7168,112]{0,1:T(8,128)(2,1)} copy(bf16[7168,112]{1,0:T(8,128)(2,1)} %bitcast.5) | data formatting | bytes 3211264
  (17 shorter events, 0.3 us)
Async XLA Ops:
  0.6 15.2 %copy-start = (bf16[64,3584]{1,0:T(8,128)(2,1)S(1)}, bf16[64,3584]{1,0:T(8,128)(2,1)}, u32[]{:S(2)}) copy-start(bf16[64,3584]{1,0:T(8,128)(2,1)} %param.13) | copy-start | bytes 1376260
  2.0 23.8 %all-to-all-start.6 = ((bf16[64,1,112]{2,1,0:T(2,128)(2,1)}), bf16[64,1,112]{2,1,0:T(2,128)(2,1)S(1)}, u32[]{:S(2)}, u32[]{:S(2)}) async-start(bf16[64,1,112]{2,1,0:T(2,128)(2,1)} %broadcast_in_dim.11), calls=%async_computation.6 | async-start | bytes 65536 | tf_op jit(solution)/shard_map/all_to_all | solution.py:14
  15.8 17.8 %copy-start.1 = (bf16[224,3584]{1,0:T(8,128)(2,1)S(1)}, bf16[224,3584]{1,0:T(8,128)(2,1)}, u32[]{:S(2)}) copy-start(bf16[224,3584]{1,0:T(8,128)(2,1)} %param.14) | copy-start | bytes 4816900
  15.8 17.8 %copy-start.2 = (bf16[64,3584]{1,0:T(8,128)(2,1)S(1)}, bf16[64,3584]{1,0:T(8,128)(2,1)}, u32[]{:S(2)}) copy-start(bf16[64,3584]{1,0:T(8,128)(2,1)} %param.16) | copy-start | bytes 1376260
  15.8 17.8 %copy-start.3 = (bf16[224,64]{0,1:T(8,128)(2,1)S(1)}, bf16[224,64]{0,1:T(8,128)(2,1)}, u32[]{:S(2)}) copy-start(bf16[224,64]{0,1:T(8,128)(2,1)} %param.15) | copy-start | bytes 86020
  25.8 21.7 %all-to-all-start = ((bf16[32,2,1792]{2,1,0:T(2,128)(2,1)}), bf16[32,2,1792]{2,1,0:T(2,128)(2,1)S(1)}, u32[]{:S(2)}, u32[]{:S(2)}) async-start(bf16[32,2,1792]{2,1,0:T(2,128)(2,1)} %reshape.74), calls=%async_computation | async-start | bytes 458752 | tf_op jit(solution)/shard_map/all_to_all | solution.py:14
  33.6 19.0 %copy-start.4 = (bf16[224,64]{0,1:T(8,128)(2,1)S(1)}, bf16[224,64]{0,1:T(8,128)(2,1)}, u32[]{:S(2)}) copy-start(bf16[224,64]{0,1:T(8,128)(2,1)} %param.18) | copy-start | bytes 86020
  47.5 18.6 %all-to-all-start.2 = ((bf16[32,2,1792]{2,1,0:T(2,128)(2,1)}), bf16[32,2,1792]{2,1,0:T(2,128)(2,1)S(1)}, u32[]{:S(2)}, u32[]{:S(2)}) async-start(bf16[32,2,1792]{2,1,0:T(2,128)(2,1)} %reshape.76), calls=%async_computation.2 | async-start | bytes 458752 | tf_op jit(solution)/shard_map/all_to_all | solution.py:14
  66.1 18.8 %all-to-all-start.4 = ((bf16[32,2,1792]{2,1,0:T(2,128)(2,1)}), bf16[32,2,1792]{2,1,0:T(2,128)(2,1)S(1)}, u32[]{:S(2)}, u32[]{:S(2)}) async-start(bf16[32,2,1792]{2,1,0:T(2,128)(2,1)} %reshape.78), calls=%async_computation.4 | async-start | bytes 458752 | tf_op jit(solution)/shard_map/all_to_all | solution.py:14
  84.9 52.8 %all-to-all-start.1 = ((bf16[224,32,112]{2,0,1:T(8,128)(2,1)}), bf16[224,32,112]{2,0,1:T(8,128)(2,1)S(1)}, u32[]{:S(2)}, u32[]{:S(2)}) async-start(bf16[224,32,112]{2,0,1:T(8,128)(2,1)} %copy.46), calls=%async_computation.1 | async-start | bytes 3670016 | tf_op jit(solution)/shard_map/all_to_all | solution.py:76
  137.7 55.4 %all-to-all-start.3 = ((bf16[224,32,112]{2,0,1:T(8,128)(2,1)}), bf16[224,32,112]{2,0,1:T(8,128)(2,1)}, u32[]{:S(2)}, u32[]{:S(2)}) async-start(bf16[224,32,112]{2,0,1:T(8,128)(2,1)} %copy.48), calls=%async_computation.3 | async-start | bytes 3670016 | tf_op jit(solution)/shard_map/all_to_all | solution.py:77
  193.1 37.5 %all-to-all-start.5 = ((bf16[224,32,112]{2,0,1:T(8,128)(2,1)}), bf16[224,32,112]{2,0,1:T(8,128)(2,1)}, u32[]{:S(2)}, u32[]{:S(2)}) async-start(bf16[224,32,112]{2,0,1:T(8,128)(2,1)} %copy.50), calls=%async_computation.5 | async-start | bytes 3670016 | tf_op jit(solution)/shard_map/all_to_all | solution.py:78
where the time goes:
time: 235 us; the launch traced here: 234 us
  waiting for transfers between devices  110 us (47%)
  starting transfers between devices  56.5 us (24%)
  local copies, waits for them, and re-layouts  39.8 us (17%)
  other arithmetic  16.7 us (7%)
  matrix products  10.2 us (4%)
    all_to_all x1, waiting for transfers between devices, shards(): lax.all_to_all(narrow_key, 'zero', split_axis=1, concat_axis=0, tiled=True)  38.8 us
    all_to_all x1, waiting for transfers between devices, shards(): lax.all_to_all(narrow_query, 'zero', split_axis=1, concat_axis=0, tiled=T...  32.5 us
    all_to_all x4, starting transfers between devices, copy_for_each(): lax.all_to_all(jnp.broadcast_to(array[None], (peers, *array.shape)), axis...  32.4 us
    all_to_all x4, waiting for transfers between devices, copy_for_each(): lax.all_to_all(jnp.broadcast_to(array[None], (peers, *array.shape)), axis...  21.4 us
    all_to_all x1, waiting for transfers between devices, shards(): lax.all_to_all(narrow_value, 'zero', split_axis=1, concat_axis=0, tiled=T...  17.5 us
    unnamed x19, local copies, waits for them, and re-layouts  13.2 us
    all_to_all x1, starting transfers between devices, shards(): lax.all_to_all(narrow_value, 'zero', split_axis=1, concat_axis=0, tiled=T...  10.8 us
    all_to_all x1, starting transfers between devices, shards(): lax.all_to_all(narrow_query, 'zero', split_axis=1, concat_axis=0, tiled=T...  8.56 us
  transfers between devices with their start and end apart: 7, of which 7 were waited for; matrix products, arithmetic and copies ran while one was open for 21% of the time, Pallas kernels for 0%

commit v1 on v0

v1 whole, which is shorter than its diff:
```python
import functools

import jax
import jax.numpy as jnp
from jax import lax
from jax.experimental import pallas as pl
from jax.experimental.pallas import tpu as pltpu
from jax.sharding import PartitionSpec as P

D_MODEL = 7168
MIX_RATE = 1.0
ROWS = 224
COLS = 3584
OWN = 112
RANK = 64
PEERS = 32
HALF = PEERS // 2
BLOCK = 200
BASE = 88
SPILL = OWN - BASE
MESH = pl.DeviceIdType.MESH
VMEM_LIMIT = 56 << 20


def unit_of_lane(rows):
    return lax.broadcasted_iota(jnp.int32, (rows, 128), 1) // 32


def packed(block, free):
    first, tail = block[:, :128], block[:, 128:]
    spill = tail[BASE:]
    moved = jnp.concatenate(
        [pltpu.roll(spill, 128 - 32 * i, axis=1) for i in (1, 2, 3)], axis=0
    )
    holds = 3 * SPILL
    mixed = jnp.where(unit_of_lane(holds) == free, moved, tail[:holds])
    return jnp.concatenate([first, mixed, tail[holds:BASE]], axis=0)


def unpacked(block, free):
    first, base = block[:OWN], block[OWN:]
    unit = unit_of_lane(SPILL)
    spill = jnp.zeros((SPILL, 128), jnp.float32)
    for i in (1, 2, 3):
        piece = pltpu.roll(base[SPILL * (i - 1) : SPILL * i], 32 * i, axis=1)
        spill = jnp.where(unit == (free + i) % 4, piece, spill)
    return first, jnp.concatenate([base, spill], axis=0)


def gather_columns(received, sums, joined, groups):
    lane = lax.broadcasted_iota(jnp.int32, (OWN, 128), 1)

    def step(i, total):
        group = groups(i)
        at = pl.multiple_of(group * 896, 128)
        parts = [
            unpacked(received[group * 4 + b].astype(jnp.float32), 3 - b) for b in range(4)
        ]
        tiles = []
        for b in range(4):
            tiles.append(parts[b][0])
            if b < 3:
                tiles.append(jnp.where(lane < 96 - 32 * b, parts[b][1], parts[b + 1][1]))
        for t, tile in enumerate(tiles):
            joined[:, pl.ds(at + 128 * t, 128)] = tile.astype(jnp.bfloat16)
            total = total + jnp.abs(tile)
        return total

    sums[...] = lax.fori_loop(0, 4, step, sums[...])


def scaled(joined, sums, final):
    scale = jnp.sum(sums[...], axis=1, keepdims=True) / D_MODEL
    factor = jnp.broadcast_to(1.0 / scale, (OWN, 896))

    def step(i, carry):
        at = pl.multiple_of(i * 896, 128)
        part = joined[:, pl.ds(at, 896)].astype(jnp.float32) * factor
        final[:, pl.ds(at, 896)] = part.astype(jnp.bfloat16)
        return carry

    lax.fori_loop(0, 8, step, 0)


def as_row(sums):
    scale = jnp.broadcast_to(
        jnp.sum(sums[...], axis=1, keepdims=True) / D_MODEL, (OWN, OWN)
    )
    row = lax.broadcasted_iota(jnp.int32, (OWN, OWN), 0)
    column = lax.broadcasted_iota(jnp.int32, (OWN, OWN), 1)
    return jnp.sum(jnp.where(row == column, scale, 0.0), axis=0, keepdims=True)


def exchange(
    train_q, low_q, high_q, train_k, low_k, high_k, train_v, low_v, high_v, norm, step,
    joined_q, joined_k, joined_v, sums_q, sums_k, sums_v, gains,
    train, low, high, result, outgoing, received,
    load_sem, send_sem, recv_sem, gain_send, gain_recv, pair_send, pair_recv,
):
    me = lax.axis_index("zero")
    width = lax.axis_index("width")
    site = lax.axis_index("site")
    far, y, x = me // 16, (me // 4) % 4, me % 4
    turn = me % 4
    sources = ((train_q, low_q, high_q), (train_k, low_k, high_k), (train_v, low_v, high_v))

    loads = []
    for m, refs in enumerate(sources):
        for part, (ref, buffer) in enumerate(zip(refs, (train, low, high), strict=True)):
            loads.append(pltpu.make_async_copy(ref, buffer.at[m], load_sem.at[m, part]))
            loads[-1].start()

    barrier = pltpu.get_barrier_semaphore()

    def greet(i, carry):
        peer = (me + i) % PEERS
        pl.semaphore_signal(barrier, inc=1, device_id=(peer, width, site), device_id_type=MESH)
        return carry

    lax.fori_loop(1, PEERS, greet, 0)
    partner = (me, 1 - width, site)
    pl.semaphore_signal(barrier, inc=1, device_id=partner, device_id_type=MESH)

    gain = (norm[...] + step[...]).astype(jnp.bfloat16).astype(jnp.float32)
    gains[me, pl.ds(width, 1), :] = jnp.concatenate(
        [gain, jnp.zeros((1, 128 - OWN), jnp.float32)], axis=1
    )

    from_row = lax.broadcasted_iota(jnp.int32, (ROWS, 256), 0)
    to_lane = lax.broadcasted_iota(jnp.int32, (ROWS, 256), 1)
    place = jnp.where(from_row == (to_lane + 32 * turn) % 256, 1.0, 0.0).astype(jnp.bfloat16)

    def merge(m, half):
        base = half * (COLS // 2)
        turned_low = jnp.dot(low[m], place, preferred_element_type=jnp.float32).astype(
            jnp.bfloat16
        )

        def columns(c, carry):
            at = pl.multiple_of(base + c * 256, 128)
            dims = (((0,), (0,)), ((), ()))
            part = lax.dot_general(
                train[m, :, pl.ds(at, 256)], place, dims, preferred_element_type=jnp.float32
            )
            part = part + MIX_RATE * lax.dot_general(
                high[m, :, pl.ds(at, 256)], turned_low, dims, preferred_element_type=jnp.float32
            )
            result[pl.ds(pl.multiple_of(c * 256, 256), 256), :] = part
            return carry

        lax.fori_loop(0, COLS // 512, columns, 0)

        def block(j, carry):
            part = result[pl.ds(pl.multiple_of(j * OWN, 8), OWN), :]
            outgoing[m, half * HALF + j] = packed(part, 3 - turn).astype(jnp.bfloat16)
            return carry

        lax.fori_loop(0, HALF, block, 0)

    def send(m, peer, sem):
        pltpu.make_async_remote_copy(
            src_ref=outgoing.at[m, peer],
            dst_ref=received.at[m, me],
            send_sem=send_sem.at[m],
            recv_sem=recv_sem.at[m, sem],
            device_id=(peer, width, site),
            device_id_type=MESH,
        ).start()

    def relative(half, i):
        return half * HALF + ((y + i // 4) % 4) * 4 + (x + i % 4) % 4

    for m in range(3):
        for part in range(3):
            loads[3 * m + part].wait()
        merge(m, 1 - far)
        if m == 0:
            pl.semaphore_wait(barrier, PEERS)
            pltpu.make_async_remote_copy(
                src_ref=gains.at[me, pl.ds(width, 1)],
                dst_ref=gains.at[me, pl.ds(width, 1)],
                send_sem=pair_send,
                recv_sem=pair_recv,
                device_id=partner,
                device_id_type=MESH,
            ).start()

        def over(i, carry, m=m):
            send(m, relative(1 - far, i), 0)
            return carry

        lax.fori_loop(0, HALF, over, 0)
        merge(m, far)

        def near(i, carry, m=m):
            send(m, relative(far, i), 1)
            return carry

        lax.fori_loop(1, HALF, near, 0)
        received[m, me] = outgoing[m, me]

    pair = pltpu.make_async_remote_copy(
        src_ref=gains.at[me, pl.ds(width, 1)],
        dst_ref=gains.at[me, pl.ds(1 - width, 1)],
        send_sem=pair_send,
        recv_sem=pair_recv,
        device_id=partner,
        device_id_type=MESH,
    )
    pair.wait_recv()

    def spread(i, carry):
        pltpu.make_async_remote_copy(
            src_ref=gains.at[me],
            dst_ref=gains.at[me],
            send_sem=gain_send,
            recv_sem=gain_recv,
            device_id=((me + i) % PEERS, width, site),
            device_id_type=MESH,
        ).start()
        return carry

    lax.fori_loop(1, PEERS, spread, 0)

    def arrived(m, sem, blocks):
        window = received.at[m, pl.ds(0, blocks)]
        pltpu.make_async_copy(window, window, recv_sem.at[m, sem]).wait()

    for m, (joined, sums) in enumerate(
        ((joined_q, sums_q), (joined_k, sums_k), (joined_v, sums_v))
    ):
        sums[...] = jnp.zeros_like(sums)
        arrived(m, 1, HALF - 1)
        gather_columns(received.at[m], sums, joined, lambda i: far * 4 + i)
        arrived(m, 0, HALF)
        gather_columns(received.at[m], sums, joined, lambda i: (1 - far) * 4 + i)
        if m < 2:
            scaled(joined, sums, joined)

    rest = gains.at[pl.ds(0, PEERS - 1)]
    pltpu.make_async_copy(rest, rest, gain_recv).wait()
    pltpu.make_async_copy(rest, rest, gain_send).wait()
    pair.wait_send()
    for m in range(3):
        window = outgoing.at[m, pl.ds(0, PEERS - 1)]
        pltpu.make_async_copy(window, window, send_sem.at[m]).wait()


def finish(
    joined_q, joined_k, joined_v, sums_q, sums_k, sums_v, gains,
    final_q, final_k, final_v, scale_q, scale_k, scale_v, serve,
    last, rows, sem,
):
    copies = [
        pltpu.make_async_copy(joined_q, final_q, sem.at[0]),
        pltpu.make_async_copy(joined_k, final_k, sem.at[1]),
        pltpu.make_async_copy(last, final_v, sem.at[2]),
    ]
    copies[0].start()
    copies[1].start()
    scaled(joined_v, sums_v, last)
    copies[2].start()
    for sums, scale in ((sums_q, scale_q), (sums_k, scale_k), (sums_v, scale_v)):
        scale[...] = as_row(sums)
    lane = lax.broadcasted_iota(jnp.int32, (1, 128), 1)
    for r in range(D_MODEL // 128):
        group, place = r // 7 * 8, r % 7
        left = gains[pl.ds(group + place, 1), :]
        right = gains[pl.ds(group + place + 1, 1), :]
        if place:
            left = pltpu.roll(left, 128 - 16 * place, axis=1)
        right = pltpu.roll(right, OWN - 16 * place, axis=1)
        rows[pl.ds(r, 1), :] = jnp.where(lane < OWN - 16 * place, left, right)
    serve[...] = rows[...].astype(jnp.bfloat16)
    for copy in copies:
        copy.wait()


def shards(
    train_query, low_query, high_query,
    train_key, low_key, high_key,
    train_value, low_value, high_value,
    norm_train, norm_step,
):
    anywhere = pl.BlockSpec(memory_space=pl.ANY)
    vmem = pl.BlockSpec(memory_space=pltpu.VMEM)
    whole = jax.ShapeDtypeStruct((OWN, D_MODEL), jnp.bfloat16)
    lanes = jax.ShapeDtypeStruct((OWN, 128), jnp.float32)
    dma = pltpu.SemaphoreType.DMA
    *middle, gains = pl.pallas_call(
        exchange,
        name="exchange",
        out_shape=(
            *[whole] * 3, *[lanes] * 3, jax.ShapeDtypeStruct((PEERS, 2, 128), jnp.float32),
        ),
        in_specs=[anywhere] * 9 + [vmem] * 2,
        out_specs=(vmem,) * 7,
        scratch_shapes=[
            pltpu.VMEM((3, ROWS, COLS), jnp.bfloat16),
            pltpu.VMEM((3, RANK, ROWS), jnp.bfloat16),
            pltpu.VMEM((3, RANK, COLS), jnp.bfloat16),
            pltpu.VMEM((COLS // 2, 256), jnp.float32),
            pltpu.VMEM((3, PEERS, BLOCK, 128), jnp.bfloat16),
            pltpu.VMEM((3, PEERS, BLOCK, 128), jnp.bfloat16),
            dma((3, 3)), dma((3,)), dma((3, 2)), dma, dma, dma, dma,
        ],
        compiler_params=pltpu.CompilerParams(
            collective_id=0, has_side_effects=True, vmem_limit_bytes=VMEM_LIMIT
        ),
    )(
        train_query, low_query.T, high_query,
        train_key, low_key.T, high_key,
        train_value, low_value.T, high_value,
        norm_train.reshape(1, OWN), norm_step.reshape(1, OWN),
    )
    *finals, scale_q, scale_k, scale_v, serve = pl.pallas_call(
        finish,
        name="finish",
        out_shape=(
            *[whole] * 3,
            *[jax.ShapeDtypeStruct((1, OWN), jnp.float32)] * 3,
            jax.ShapeDtypeStruct((D_MODEL // 128, 128), jnp.bfloat16),
        ),
        in_specs=[vmem] * 7,
        out_specs=(anywhere,) * 3 + (vmem,) * 4,
        scratch_shapes=[
            pltpu.VMEM((OWN, D_MODEL), jnp.bfloat16),
            pltpu.VMEM((D_MODEL // 128, 128), jnp.float32),
            dma((3,)),
        ],
        compiler_params=pltpu.CompilerParams(vmem_limit_bytes=16 << 20),
    )(*middle, gains.reshape(2 * PEERS, 128))
    return (
        *[final.T for final in finals],
        scale_q.reshape(OWN), scale_k.reshape(OWN), scale_v.reshape(OWN),
        serve.reshape(D_MODEL),
    )


def solution(mesh):
    weights = (P(("site", "zero"), "width"), P(("site", "zero"), None), P("site", "width"))
    gain = P(("site", "zero", "width"))
    return jax.shard_map(
        shards,
        mesh=mesh,
        in_specs=weights * 3 + (gain, gain),
        out_specs=(P("site", ("width", "zero")),) * 3
        + (P(("site", "width", "zero")),) * 3
        + (P("site"),),
        check_vma=False,
    )
```

time: 235 us -> 139 us (0.59)
  the two profiles are of different devices: /device:TPU:64 before, /device:TPU:1 now
where the time goes in v1:
time: 139 us; the launch traced here: 138 us
  Pallas kernels  130 us (94%)
  local copies, waits for them, and re-layouts  7.46 us (5%)
    pallas_call x1, Pallas kernels, shards(): pl.pallas_call(exchange, name='exchange', out_shape=(*[whole] * 3, *[lane...  127 us
    unnamed x14, local copies, waits for them, and re-layouts  7.46 us
    pallas_call x1, Pallas kernels, shards(): pl.pallas_call(finish, name='finish', out_shape=(*[whole] * 3, *[jax.Shap...  2.85 us

profile of v1, /device:TPU:1, one launch (start us, length us, event | category | flops | bytes accessed | tf_op | source)
XLA Modules:
  0.0 138.1 jit_solution(13057572889988520126)
XLA Ops:
  0.6 127.2 %exchange.1 = (bf16[112,7168]{1,0:T(8,128)(2,1)}, bf16[112,7168]{1,0:T(8,128)(2,1)}, bf16[112,7168]{1,0:T(8,128)(2,1)}, f32[112,128]{1,0:T(8,128)}, f32[112,128]...) custom-call(bf16[224,3584]{1,0:T(8,128)(2,1)} %train_q.1, bf16[64,224]{1,0:T(8,128)(2,1)} %bitcast.14, ...), custom_call_target="tpu_custom_call" | custom-call | tf_op jit(solution)/shard_map/exchange/pallas_call | solution.py:290
  127.8 0.0 copy-start
  127.8 1.4 %copy-done = bf16[112,7168]{1,0:T(8,128)(2,1)S(1)} copy-done((bf16[112,7168]{1,0:T(8,128)(2,1)S(1)}, bf16[112,7168]{1,0:T(8,128)(2,1)}, u32[]{:S(2)}) %copy-start) | copy-done | bytes 1605656
  129.2 0.0 copy-start.1
  129.2 1.4 %copy-done.1 = bf16[112,7168]{1,0:T(8,128)(2,1)S(1)} copy-done((bf16[112,7168]{1,0:T(8,128)(2,1)S(1)}, bf16[112,7168]{1,0:T(8,128)(2,1)}, u32[]{:S(2)}) %copy-start.1) | copy-done | bytes 1605656
  130.6 0.0 copy-start.2
  130.6 1.4 %copy-done.2 = bf16[112,7168]{1,0:T(8,128)(2,1)S(1)} copy-done((bf16[112,7168]{1,0:T(8,128)(2,1)S(1)}, bf16[112,7168]{1,0:T(8,128)(2,1)}, u32[]{:S(2)}) %copy-start.2) | copy-done | bytes 1605656
  132.1 0.0 copy-start.3
  132.1 0.8 copy-done.3
  132.9 0.0 copy-start.4
  132.9 0.8 copy-done.4
  133.7 0.0 copy-start.5
  133.7 0.8 copy-done.5
  134.5 0.0 copy-start.6
  134.5 0.8 copy-done.6
  135.3 2.8 %finish.1 = (bf16[112,7168]{1,0:T(8,128)(2,1)}, bf16[112,7168]{1,0:T(8,128)(2,1)}, bf16[112,7168]{1,0:T(8,128)(2,1)}, f32[1,112]{1,0:T(1,128)}, f32[1,112]{1,0:T...) custom-call(bf16[112,7168]{1,0:T(8,128)(2,1)S(1)} %copy-done, bf16[112,7168]{1,0:T(8,128)(2,1)S(1)} %copy-done.1, ...), custom_call_target="tpu_custom_call" | custom-call | tf_op jit(solution)/shard_map/finish/pallas_call | solution.py:316
Async XLA Ops:
  127.8 1.4 %copy-start = (bf16[112,7168]{1,0:T(8,128)(2,1)S(1)}, bf16[112,7168]{1,0:T(8,128)(2,1)}, u32[]{:S(2)}) copy-start(bf16[112,7168]{1,0:T(8,128)(2,1)} %get-tuple-element.21.joined_q) | copy-start | bytes 4816900
  129.2 1.4 %copy-start.1 = (bf16[112,7168]{1,0:T(8,128)(2,1)S(1)}, bf16[112,7168]{1,0:T(8,128)(2,1)}, u32[]{:S(2)}) copy-start(bf16[112,7168]{1,0:T(8,128)(2,1)} %get-tuple-element.22.joined_k) | copy-start | bytes 4816900
  130.6 1.4 %copy-start.2 = (bf16[112,7168]{1,0:T(8,128)(2,1)S(1)}, bf16[112,7168]{1,0:T(8,128)(2,1)}, u32[]{:S(2)}) copy-start(bf16[112,7168]{1,0:T(8,128)(2,1)} %get-tuple-element.23.joined_v) | copy-start | bytes 4816900
  132.1 0.8 copy-start.3
  132.9 0.8 copy-start.4
  133.7 0.8 copy-start.5
  134.5 0.8 copy-start.6

commit v2 on v1

--- a/solution.py
+++ b/solution.py
@@ -285,13 +285,14 @@
     anywhere = pl.BlockSpec(memory_space=pl.ANY)
     vmem = pl.BlockSpec(memory_space=pltpu.VMEM)
     whole = jax.ShapeDtypeStruct((OWN, D_MODEL), jnp.bfloat16)
-    lanes = jax.ShapeDtypeStruct((OWN, 128), jnp.float32)
+    held = pltpu.VMEM((OWN, D_MODEL), jnp.bfloat16)
+    lanes = pltpu.VMEM((OWN, 128), jnp.float32)
     dma = pltpu.SemaphoreType.DMA
     *middle, gains = pl.pallas_call(
         exchange,
         name="exchange",
         out_shape=(
-            *[whole] * 3, *[lanes] * 3, jax.ShapeDtypeStruct((PEERS, 2, 128), jnp.float32),
+            *[held] * 3, *[lanes] * 3, pltpu.VMEM((PEERS, 2, 128), jnp.float32),
         ),
         in_specs=[anywhere] * 9 + [vmem] * 2,
         out_specs=(vmem,) * 7,

time: 139 us -> 129 us (0.928)
  local copies, waits for them, and re-layouts: 7.46 us -> 0 us
  Pallas kernels: 130 us -> 128 us
    unnamed x14 -> x0, local copies, waits for them, and re-layouts: 7.46 us -> none
    pallas_call x1, Pallas kernels: 127 us -> 125 us  [shards(): pl.pallas_call(exchange, name='exchange', out_shape=(*[held] * 3, *[lanes...]
where the time goes in v2:
time: 129 us; the launch traced here: 128 us
  Pallas kernels  128 us (99%)
    pallas_call x1, Pallas kernels, shards(): pl.pallas_call(exchange, name='exchange', out_shape=(*[held] * 3, *[lanes...  125 us
    pallas_call x1, Pallas kernels, shards(): pl.pallas_call(finish, name='finish', out_shape=(*[whole] * 3, *[jax.Shap...  2.85 us

profile of v2, /device:TPU:1, one launch (start us, length us, event | category | flops | bytes accessed | tf_op | source)
XLA Modules:
  0.0 128.4 jit_solution(7913651396529965162)
XLA Ops:
  0.6 125.0 %exchange.1 = (bf16[112,7168]{1,0:T(8,128)(2,1)S(1)}, bf16[112,7168]{1,0:T(8,128)(2,1)S(1)}, bf16[112,7168]{1,0:T(8,128)(2,1)S(1)}, f32[112,128]{1,0:T(8,128)S(1...) custom-call(bf16[224,3584]{1,0:T(8,128)(2,1)} %train_q.1, bf16[64,224]{1,0:T(8,128)(2,1)} %bitcast.14, ...), custom_call_target="tpu_custom_call" | custom-call | tf_op jit(solution)/shard_map/exchange/pallas_call | solution.py:291
  125.6 2.9 %finish.1 = (bf16[112,7168]{1,0:T(8,128)(2,1)}, bf16[112,7168]{1,0:T(8,128)(2,1)}, bf16[112,7168]{1,0:T(8,128)(2,1)}, f32[1,112]{1,0:T(1,128)}, f32[1,112]{1,0:T...) custom-call(bf16[112,7168]{1,0:T(8,128)(2,1)S(1)} %get-tuple-element.21.joined_q, ...), custom_call_target="tpu_custom_call" | custom-call | tf_op jit(solution)/shard_map/finish/pallas_call | solution.py:317

commit v3 on v1

v3 whole, which is shorter than its diff:
```python
import functools

import jax
import jax.numpy as jnp
from jax import lax
from jax.experimental import pallas as pl
from jax.experimental.pallas import tpu as pltpu
from jax.sharding import PartitionSpec as P

D_MODEL = 7168
MIX_RATE = 1.0
ROWS = 224
COLS = 3584
OWN = 112
RANK = 64
PEERS = 32
HALF = PEERS // 2
BASE = (80, 88, 88)
BLOCK = OWN + max(BASE)
OVER = 3 * (OWN - BASE[0]) - BASE[0]
MESH = pl.DeviceIdType.MESH
VMEM_LIMIT = 56 << 20


def unit_of_lane(rows):
    return lax.broadcasted_iota(jnp.int32, (rows, 128), 1) // 32


def packed(block, free, base, more=()):
    first, tail = block[:, :128], block[:, 128:]
    spill = tail[base:]
    moved = jnp.concatenate(
        [pltpu.roll(spill, 128 - 32 * i, axis=1) for i in (1, 2, 3)] + list(more), axis=0
    )
    holds = min(base, moved.shape[0])
    mixed = jnp.where(unit_of_lane(holds) == free, moved[:holds], tail[:holds])
    rows = [first, mixed] + ([tail[holds:base]] if holds < base else [])
    rest = moved[holds:] if holds < moved.shape[0] else None
    return jnp.concatenate(rows, axis=0), rest


def unpacked(block, free, base, more=()):
    first, tail = block[:OWN], block[OWN : OWN + base]
    moved = jnp.concatenate([tail, *more], axis=0)
    size = OWN - base
    unit = unit_of_lane(size)
    spill = jnp.zeros((size, 128), jnp.float32)
    for i in (1, 2, 3):
        piece = pltpu.roll(moved[size * (i - 1) : size * i], 32 * i, axis=1)
        spill = jnp.where(unit == (free + i) % 4, piece, spill)
    return first, jnp.concatenate([tail, spill], axis=0)


def gather_columns(received, m, group, total, joined):
    lane = lax.broadcasted_iota(jnp.int32, (OWN, 128), 1)
    at = pl.multiple_of(group * 896, 128)
    parts = []
    for b in range(4):
        peer = group * 4 + b
        more = ()
        if m == 0:
            more = (received[1, peer, BLOCK - OVER :].astype(jnp.float32),)
        block = received[m, peer].astype(jnp.float32)
        parts.append(unpacked(block, 3 - b, BASE[m], more))
    tiles = []
    for b in range(4):
        tiles.append(parts[b][0])
        if b < 3:
            tiles.append(jnp.where(lane < 96 - 32 * b, parts[b][1], parts[b + 1][1]))
    for t, tile in enumerate(tiles):
        joined[:, pl.ds(at + 128 * t, 128)] = tile.astype(jnp.bfloat16)
        total = total + jnp.abs(tile)
    return total


def scale_of(sums):
    return jnp.sum(sums[...], axis=1, keepdims=True) / D_MODEL


def rescaled(joined, factor, final, i):
    window = pl.ds(pl.multiple_of(i * 896, 128), 896)
    final[:, window] = (joined[:, window].astype(jnp.float32) * factor).astype(jnp.bfloat16)


def as_row(scale):
    row = lax.broadcasted_iota(jnp.int32, (OWN, OWN), 0)
    column = lax.broadcasted_iota(jnp.int32, (OWN, OWN), 1)
    spread = jnp.broadcast_to(scale, (OWN, OWN))
    return jnp.sum(jnp.where(row == column, spread, 0.0), axis=0, keepdims=True)


def exchange(
    train_q, low_q, high_q, train_k, low_k, high_k, train_v, low_v, high_v, norm, step,
    joined_q, joined_k, joined_v, sums_v, scale_q, scale_k, serve,
    train, low, high, result, outgoing, received, sums, gains, over, rows,
    load_sem, low_sem, send_sem, recv_sem, gain_send, gain_recv, pair_send, pair_recv,
    across_send, across_recv,
):
    me = lax.axis_index("zero")
    width = lax.axis_index("width")
    site = lax.axis_index("site")
    far, y, x = me // 16, (me // 4) % 4, me % 4
    plane = me % 16
    sources = ((train_q, low_q, high_q), (train_k, low_k, high_k), (train_v, low_v, high_v))

    def group_of(s):
        return ((far + 1 + s // 2) % 2) * 2 + (y // 2 + s) % 2

    def loads(m, s):
        window = pl.ds(pl.multiple_of(group_of(s) * 896, 128), 896)
        return [
            pltpu.make_async_copy(
                sources[m][part].at[:, window], held.at[m, :, window], load_sem.at[m, s, i]
            )
            for i, (part, held) in enumerate(((0, train), (2, high)))
        ]

    def low_load(m):
        return pltpu.make_async_copy(sources[m][1], low.at[m], low_sem.at[m])

    def start_loads(m, s):
        if s == 0:
            low_load(m).start()
        for load in loads(m, s):
            load.start()

    start_loads(0, 0)
    barrier = pltpu.get_barrier_semaphore()

    def greet(i, carry):
        peer = (me + i) % PEERS
        pl.semaphore_signal(barrier, inc=1, device_id=(peer, width, site), device_id_type=MESH)
        return carry

    lax.fori_loop(1, PEERS, greet, 0)
    partner = (me, 1 - width, site)
    pl.semaphore_signal(barrier, inc=1, device_id=partner, device_id_type=MESH)
    for m in range(3):
        for s in range(4):
            if m or s:
                start_loads(m, s)

    from_row = lax.broadcasted_iota(jnp.int32, (ROWS, 256), 0)
    to_lane = lax.broadcasted_iota(jnp.int32, (ROWS, 256), 1)
    place = jnp.where(from_row == (to_lane + 32 * x) % 256, 1.0, 0.0).astype(jnp.bfloat16)

    gain = (norm[...] + step[...]).astype(jnp.bfloat16).astype(jnp.float32)
    gains[plane, far, pl.ds(width, 1), :] = jnp.concatenate(
        [gain, jnp.zeros((1, 128 - OWN), jnp.float32)], axis=1
    )

    def merge(m, group, turned_low):
        window = pl.ds(pl.multiple_of(group * 896, 128), 896)
        dims = (((0,), (0,)), ((), ()))
        result[...] = lax.dot_general(
            train[m, :, window], place, dims, preferred_element_type=jnp.float32
        ) + MIX_RATE * lax.dot_general(
            high[m, :, window], turned_low, dims, preferred_element_type=jnp.float32
        )

    def peer_of(group, j):
        return group * 8 + ((y + j // 4) % 2) * 4 + (x + j) % 4

    def pack(m, group, j):
        peer = peer_of(group, j)
        at = pl.multiple_of((peer - group * 8) * OWN, 8)
        more = (over[peer],) if m == 1 else ()
        rows_out, rest = packed(result[pl.ds(at, OWN), :], 3 - x, BASE[m], more)
        outgoing[m, peer, : OWN + BASE[m]] = rows_out.astype(jnp.bfloat16)
        if m == 0:
            over[peer] = rest

    def send(m, group, j, sem):
        peer = peer_of(group, j)

        @pl.when(peer != me)
        def _():
            pltpu.make_async_remote_copy(
                src_ref=outgoing.at[m, peer, pl.ds(0, OWN + BASE[m])],
                dst_ref=received.at[m, me, pl.ds(0, OWN + BASE[m])],
                send_sem=send_sem.at[m],
                recv_sem=recv_sem.at[m, sem],
                device_id=(peer, width, site),
                device_id_type=MESH,
            ).start()

    def across(end):
        return pltpu.make_async_remote_copy(
            src_ref=gains.at[plane, end],
            dst_ref=gains.at[plane, end],
            send_sem=across_send,
            recv_sem=across_recv,
            device_id=((me + HALF) % PEERS, width, site),
            device_id_type=MESH,
        )

    def spread(i, carry):
        pltpu.make_async_remote_copy(
            src_ref=gains.at[plane],
            dst_ref=gains.at[plane],
            send_sem=gain_send,
            recv_sem=gain_recv,
            device_id=(far * HALF + (plane + i) % HALF, width, site),
            device_id_type=MESH,
        ).start()
        return carry

    for m in range(3):
        for s in range(4):
            if s == 0:
                low_load(m).wait()
                turned_low = jnp.dot(
                    low[m], place, preferred_element_type=jnp.float32
                ).astype(jnp.bfloat16)
            for load in loads(m, s):
                load.wait()
            group = group_of(s)
            sem = y if s < 2 else 4
            merge(m, group, turned_low)
            pack(m, group, 0)
            if m == 0 and s == 0:
                pl.semaphore_wait(barrier, PEERS)

            def pack_and_send(j, carry, m=m, group=group, sem=sem):
                pack(m, group, j)
                send(m, group, j - 1, sem)
                return carry

            lax.fori_loop(1, 8, pack_and_send, 0)
            send(m, group, 7, sem)
            if m == 0 and s == 0:
                pltpu.make_async_remote_copy(
                    src_ref=gains.at[plane, far, pl.ds(width, 1)],
                    dst_ref=gains.at[plane, far, pl.ds(width, 1)],
                    send_sem=pair_send,
                    recv_sem=pair_recv,
                    device_id=partner,
                    device_id_type=MESH,
                ).start()
        if m == 0:
            pair = pltpu.make_async_remote_copy(
                src_ref=gains.at[plane, far, pl.ds(width, 1)],
                dst_ref=gains.at[plane, far, pl.ds(1 - width, 1)],
                send_sem=pair_send,
                recv_sem=pair_recv,
                device_id=partner,
                device_id_type=MESH,
            )
            pair.wait_recv()

            across(far).start()
        received[m, me] = outgoing[m, me]

    across(1 - far).wait_recv()
    lax.fori_loop(1, HALF, spread, 0)

    def arrived(m, sem, blocks):
        window = received.at[m, pl.ds(0, blocks), pl.ds(0, OWN + BASE[m])]
        pltpu.make_async_copy(window, window, recv_sem.at[m, sem]).wait()

    def gather_near(m, joined):
        if m == 2:
            arrived(m, 4, HALF - 1)
        sums[...] = lax.fori_loop(
            0,
            4,
            lambda i, total: gather_columns(received, m, far * 4 + i, total, joined),
            jnp.zeros((OWN, 128), jnp.float32),
        )

    def gather_far(m, joined):
        def one(i, carry):
            row = (y // 2 * 2 + (y + i) % 2 + i // 2 * 2) % 4
            if m == 2:
                arrived(m, row, 4)
            sums[...] = gather_columns(received, m, (1 - far) * 4 + row, sums[...], joined)
            return carry

        lax.fori_loop(0, 4, one, 0)

    for m in range(2):
        for sem in range(4):
            arrived(m, sem, 4)
        arrived(m, 4, HALF - 1)
    for m, (joined, scale_row) in enumerate(((joined_q, scale_q), (joined_k, scale_k))):
        gather_near(m, joined)
        gather_far(m, joined)
        scale = scale_of(sums)
        scale_row[...] = as_row(scale)
        factor = jnp.broadcast_to(1.0 / scale, (OWN, 896))

        def rescale(i, carry, joined=joined, factor=factor):
            rescaled(joined, factor, joined, i)
            return carry

        lax.fori_loop(0, 8, rescale, 0)

    gather_near(2, joined_v)
    spread_out = gains.at[pl.ds(0, HALF - 1)]
    pltpu.make_async_copy(spread_out, spread_out, gain_recv).wait()
    pltpu.make_async_copy(spread_out, spread_out, gain_send).wait()
    pair.wait_send()
    across(far).wait_send()
    lane = lax.broadcasted_iota(jnp.int32, (1, 128), 1)
    for r in range(D_MODEL // 128):
        place_in = r % 7
        first = r // 7 * 8 + place_in
        left, right = (
            gains[i // 2 % HALF, i // 2 // HALF, pl.ds(i % 2, 1), :] for i in (first, first + 1)
        )
        if place_in:
            left = pltpu.roll(left, 128 - 16 * place_in, axis=1)
        right = pltpu.roll(right, OWN - 16 * place_in, axis=1)
        rows[pl.ds(r, 1), :] = jnp.where(lane < OWN - 16 * place_in, left, right)
    serve[...] = rows[...].astype(jnp.bfloat16)

    for m in range(2):
        window = outgoing.at[m, pl.ds(0, PEERS - 1), pl.ds(0, OWN + BASE[m])]
        pltpu.make_async_copy(window, window, send_sem.at[m]).wait()
    gather_far(2, joined_v)
    sums_v[...] = sums[...]
    window = outgoing.at[2, pl.ds(0, PEERS - 1), pl.ds(0, OWN + BASE[2])]
    pltpu.make_async_copy(window, window, send_sem.at[2]).wait()


def finish(
    joined_q, joined_k, joined_v, sums_v, row_q, row_k, gain,
    final_q, final_k, final_v, scale_q, scale_k, scale_v, serve,
    last, row_v, sem,
):
    copies = [
        pltpu.make_async_copy(source, target, sem.at[i])
        for i, (source, target) in enumerate(
            (
                (row_q, scale_q), (row_k, scale_k), (gain, serve),
                (joined_q, final_q), (joined_k, final_k),
            )
        )
    ]
    for copy in copies:
        copy.start()
    scale = scale_of(sums_v)
    factor = jnp.broadcast_to(1.0 / scale, (OWN, 896))
    row_v[...] = as_row(scale)
    for i in range(8):
        rescaled(joined_v, factor, last, i)
        window = pl.ds(896 * i, 896)
        copies.append(
            pltpu.make_async_copy(last.at[:, window], final_v.at[:, window], sem.at[5 + i])
        )
        copies[-1].start()
        if i == 0:
            copies.append(pltpu.make_async_copy(row_v, scale_v, sem.at[13]))
            copies[-1].start()
    for copy in copies:
        copy.wait()


def shards(
    train_query, low_query, high_query,
    train_key, low_key, high_key,
    train_value, low_value, high_value,
    norm_train, norm_step,
):
    anywhere = pl.BlockSpec(memory_space=pl.ANY)
    vmem = pl.BlockSpec(memory_space=pltpu.VMEM)
    whole, row = (OWN, D_MODEL), (1, OWN)
    gain = (D_MODEL // 128, 128)
    dma = pltpu.SemaphoreType.DMA
    middle = pl.pallas_call(
        exchange,
        name="exchange",
        out_shape=(
            *[pltpu.VMEM(whole, jnp.bfloat16)] * 3,
            pltpu.VMEM((OWN, 128), jnp.float32),
            *[pltpu.VMEM(row, jnp.float32)] * 2,
            pltpu.VMEM(gain, jnp.bfloat16),
        ),
        in_specs=[anywhere] * 9 + [vmem] * 2,
        out_specs=(vmem,) * 7,
        scratch_shapes=[
            pltpu.VMEM((3, ROWS, COLS), jnp.bfloat16),
            pltpu.VMEM((3, RANK, ROWS), jnp.bfloat16),
            pltpu.VMEM((3, RANK, COLS), jnp.bfloat16),
            pltpu.VMEM((896, 256), jnp.float32),
            pltpu.VMEM((3, PEERS, BLOCK, 128), jnp.bfloat16),
            pltpu.VMEM((3, PEERS, BLOCK, 128), jnp.bfloat16),
            pltpu.VMEM((OWN, 128), jnp.float32),
            pltpu.VMEM((HALF, 2, 2, 128), jnp.float32),
            pltpu.VMEM((PEERS, OVER, 128), jnp.float32),
            pltpu.VMEM(gain, jnp.float32),
            dma((3, 4, 2)), dma((3,)), dma((3,)), dma((3, 5)), *[dma] * 6,
        ],
        compiler_params=pltpu.CompilerParams(
            collective_id=0, has_side_effects=True, vmem_limit_bytes=VMEM_LIMIT
        ),
    )(
        train_query, low_query.T, high_query,
        train_key, low_key.T, high_key,
        train_value, low_value.T, high_value,
        norm_train.reshape(row), norm_step.reshape(row),
    )
    *finals, scale_q, scale_k, scale_v, serve = pl.pallas_call(
        finish,
        name="finish",
        out_shape=(
            *[jax.ShapeDtypeStruct(whole, jnp.bfloat16)] * 3,
            *[jax.ShapeDtypeStruct(row, jnp.float32)] * 3,
            jax.ShapeDtypeStruct(gain, jnp.bfloat16),
        ),
        in_specs=[vmem] * 7,
        out_specs=(anywhere,) * 7,
        scratch_shapes=[
            pltpu.VMEM(whole, jnp.bfloat16), pltpu.VMEM(row, jnp.float32), dma((14,)),
        ],
        compiler_params=pltpu.CompilerParams(vmem_limit_bytes=16 << 20),
    )(*middle)
    return (
        *[final.T for final in finals],
        scale_q.reshape(OWN), scale_k.reshape(OWN), scale_v.reshape(OWN),
        serve.reshape(D_MODEL),
    )


def solution(mesh):
    weights = (P(("site", "zero"), "width"), P(("site", "zero"), None), P("site", "width"))
    gain = P(("site", "zero", "width"))
    return jax.shard_map(
        shards,
        mesh=mesh,
        in_specs=weights * 3 + (gain, gain),
        out_specs=(P("site", ("width", "zero")),) * 3
        + (P(("site", "width", "zero")),) * 3
        + (P("site"),),
        check_vma=False,
    )
```

time: 139 us -> 123 us (0.88)
  the two profiles are of different devices: /device:TPU:1 before, /device:TPU:64 now
where the time goes in v3:
time: 123 us; the launch traced here: 122 us
  Pallas kernels  121 us (98%)
    pallas_call x1, Pallas kernels, shards(): pl.pallas_call(exchange, name='exchange', out_shape=(*[pltpu.VMEM(whole,...  119 us

profile of v3, /device:TPU:64, one launch (start us, length us, event | category | flops | bytes accessed | tf_op | source)
XLA Modules:
  0.0 121.7 jit_solution(13791176973236328040)
XLA Ops:
  0.6 118.7 %exchange.1 = (bf16[112,7168]{1,0:T(8,128)(2,1)S(1)}, bf16[112,7168]{1,0:T(8,128)(2,1)S(1)}, bf16[112,7168]{1,0:T(8,128)(2,1)S(1)}, f32[112,128]{1,0:T(8,128)S(1...) custom-call(bf16[224,3584]{1,0:T(8,128)(2,1)} %train_q.1, bf16[64,224]{1,0:T(8,128)(2,1)} %bitcast.12, ...), custom_call_target="tpu_custom_call" | custom-call | tf_op jit(solution)/shard_map/exchange/pallas_call | solution.py:370
  119.4 2.3 %finish.1 = (bf16[112,7168]{1,0:T(8,128)(2,1)}, bf16[112,7168]{1,0:T(8,128)(2,1)}, bf16[112,7168]{1,0:T(8,128)(2,1)}, f32[1,112]{1,0:T(1,128)}, f32[1,112]{1,0:T...) custom-call(bf16[112,7168]{1,0:T(8,128)(2,1)S(1)} %get-tuple-element.21.joined_q, ...), custom_call_target="tpu_custom_call" | custom-call | tf_op jit(solution)/shard_map/finish/pallas_call | solution.py:403

commit v4 on v3

--- a/solution.py
+++ b/solution.py
@@ -18,6 +18,10 @@
 BASE = (80, 88, 88)
 BLOCK = OWN + max(BASE)
 OVER = 3 * (OWN - BASE[0]) - BASE[0]
+FAR_FIRST = sorted(
+    ((dy, dx) for dy in range(4) for dx in range(4)),
+    key=lambda hop: -(min(hop[0], 4 - hop[0]) + min(hop[1], 4 - hop[1])),
+)
 MESH = pl.DeviceIdType.MESH
 VMEM_LIMIT = 56 << 20
 
@@ -158,31 +162,25 @@
             high[m, :, window], turned_low, dims, preferred_element_type=jnp.float32
         )
 
-    def peer_of(group, j):
-        return group * 8 + ((y + j // 4) % 2) * 4 + (x + j) % 4
-
     def pack(m, group, j):
-        peer = peer_of(group, j)
-        at = pl.multiple_of((peer - group * 8) * OWN, 8)
+        peer = group * 8 + j
+        at = pl.multiple_of(j * OWN, 8)
         more = (over[peer],) if m == 1 else ()
         rows_out, rest = packed(result[pl.ds(at, OWN), :], 3 - x, BASE[m], more)
         outgoing[m, peer, : OWN + BASE[m]] = rows_out.astype(jnp.bfloat16)
         if m == 0:
             over[peer] = rest
 
-    def send(m, group, j, sem):
-        peer = peer_of(group, j)
-
-        @pl.when(peer != me)
-        def _():
-            pltpu.make_async_remote_copy(
-                src_ref=outgoing.at[m, peer, pl.ds(0, OWN + BASE[m])],
-                dst_ref=received.at[m, me, pl.ds(0, OWN + BASE[m])],
-                send_sem=send_sem.at[m],
-                recv_sem=recv_sem.at[m, sem],
-                device_id=(peer, width, site),
-                device_id_type=MESH,
-            ).start()
+    def send(m, plane_z, dy, dx, sem):
+        peer = plane_z * HALF + (y + dy) % 4 * 4 + (x + dx) % 4
+        pltpu.make_async_remote_copy(
+            src_ref=outgoing.at[m, peer, pl.ds(0, OWN + BASE[m])],
+            dst_ref=received.at[m, me, pl.ds(0, OWN + BASE[m])],
+            send_sem=send_sem.at[m],
+            recv_sem=recv_sem.at[m, sem],
+            device_id=(peer, width, site),
+            device_id_type=MESH,
+        ).start()
 
     def across(end):
         return pltpu.make_async_remote_copy(
@@ -215,20 +213,23 @@
             for load in loads(m, s):
                 load.wait()
             group = group_of(s)
-            sem = y if s < 2 else 4
             merge(m, group, turned_low)
-            pack(m, group, 0)
-            if m == 0 and s == 0:
+
+            def pack_one(j, carry, m=m, group=group):
+                pack(m, group, j)
+                return carry
+
+            lax.fori_loop(0, 8, pack_one, 0)
+            if s % 2 == 0:
+                continue
+            if m == 0 and s == 1:
                 pl.semaphore_wait(barrier, PEERS)
-
-            def pack_and_send(j, carry, m=m, group=group, sem=sem):
-                pack(m, group, j)
-                send(m, group, j - 1, sem)
-                return carry
-
-            lax.fori_loop(1, 8, pack_and_send, 0)
-            send(m, group, 7, sem)
-            if m == 0 and s == 0:
+            for dy, dx in FAR_FIRST:
+                if s == 1:
+                    send(m, 1 - far, dy, dx, y)
+                elif dy or dx:
+                    send(m, far, dy, dx, 4)
+            if m == 0 and s == 1:
                 pltpu.make_async_remote_copy(
                     src_ref=gains.at[plane, far, pl.ds(width, 1)],
                     dst_ref=gains.at[plane, far, pl.ds(width, 1)],
@@ -270,7 +271,7 @@
 
     def gather_far(m, joined):
         def one(i, carry):
-            row = (y // 2 * 2 + (y + i) % 2 + i // 2 * 2) % 4
+            row = (y + 2 - i % 2 + i // 2 * 2) % 4
             if m == 2:
                 arrived(m, row, 4)
             sums[...] = gather_columns(received, m, (1 - far) * 4 + row, sums[...], joined)

time: 123 us -> 122 us (level)
    pallas_call x1, Pallas kernels: 119 us -> 117 us  [shards(): pl.pallas_call(exchange, name='exchange', out_shape=(*[pltpu.VMEM(whole,...]
where the time goes in v4:
time: 122 us; the launch traced here: 120 us
  Pallas kernels  120 us (98%)
    pallas_call x1, Pallas kernels, shards(): pl.pallas_call(exchange, name='exchange', out_shape=(*[pltpu.VMEM(whole,...  117 us

profile of v4, /device:TPU:64, one launch (start us, length us, event | category | flops | bytes accessed | tf_op | source)
XLA Modules:
  0.0 120.4 jit_solution(4168839342632529757)
XLA Ops:
  0.6 117.4 %exchange.1 = (bf16[112,7168]{1,0:T(8,128)(2,1)S(1)}, bf16[112,7168]{1,0:T(8,128)(2,1)S(1)}, bf16[112,7168]{1,0:T(8,128)(2,1)S(1)}, f32[112,128]{1,0:T(8,128)S(1...) custom-call(bf16[224,3584]{1,0:T(8,128)(2,1)} %train_q.1, bf16[64,224]{1,0:T(8,128)(2,1)} %bitcast.12, ...), custom_call_target="tpu_custom_call" | custom-call | tf_op jit(solution)/shard_map/exchange/pallas_call | solution.py:371
  118.1 2.3 %finish.1 = (bf16[112,7168]{1,0:T(8,128)(2,1)}, bf16[112,7168]{1,0:T(8,128)(2,1)}, bf16[112,7168]{1,0:T(8,128)(2,1)}, f32[1,112]{1,0:T(1,128)}, f32[1,112]{1,0:T...) custom-call(bf16[112,7168]{1,0:T(8,128)(2,1)S(1)} %get-tuple-element.21.joined_q, ...), custom_call_target="tpu_custom_call" | custom-call | tf_op jit(solution)/shard_map/finish/pallas_call | solution.py:404

commit v5 on v4

--- a/solution.py
+++ b/solution.py
@@ -204,32 +204,33 @@
         return carry
 
     for m in range(3):
-        for s in range(4):
-            if s == 0:
-                low_load(m).wait()
-                turned_low = jnp.dot(
-                    low[m], place, preferred_element_type=jnp.float32
-                ).astype(jnp.bfloat16)
+        low_load(m).wait()
+        turned_low = jnp.dot(low[m], place, preferred_element_type=jnp.float32).astype(
+            jnp.bfloat16
+        )
+
+        def prepare(s, carry, m=m, turned_low=turned_low):
             for load in loads(m, s):
                 load.wait()
             group = group_of(s)
             merge(m, group, turned_low)
 
-            def pack_one(j, carry, m=m, group=group):
+            def pack_one(j, inner):
                 pack(m, group, j)
-                return carry
-
-            lax.fori_loop(0, 8, pack_one, 0)
-            if s % 2 == 0:
-                continue
-            if m == 0 and s == 1:
+                return inner
+
+            return lax.fori_loop(0, 8, pack_one, carry)
+
+        for half in range(2):
+            lax.fori_loop(2 * half, 2 * half + 2, prepare, 0)
+            if m == 0 and half == 0:
                 pl.semaphore_wait(barrier, PEERS)
             for dy, dx in FAR_FIRST:
-                if s == 1:
+                if half == 0:
                     send(m, 1 - far, dy, dx, y)
                 elif dy or dx:
                     send(m, far, dy, dx, 4)
-            if m == 0 and s == 1:
+            if m == 0 and half == 0:
                 pltpu.make_async_remote_copy(
                     src_ref=gains.at[plane, far, pl.ds(width, 1)],
                     dst_ref=gains.at[plane, far, pl.ds(width, 1)],

time: 122 us -> 122 us (level)
  no operation moved by 1% of the time
where the time goes in v5:
time: 122 us; the launch traced here: 120 us
  Pallas kernels  120 us (98%)
    pallas_call x1, Pallas kernels, shards(): pl.pallas_call(exchange, name='exchange', out_shape=(*[pltpu.VMEM(whole,...  117 us

profile of v5, /device:TPU:64, one launch (start us, length us, event | category | flops | bytes accessed | tf_op | source)
XLA Modules:
  0.0 120.4 jit_solution(1074120031691126628)
XLA Ops:
  0.6 117.4 %exchange.1 = (bf16[112,7168]{1,0:T(8,128)(2,1)S(1)}, bf16[112,7168]{1,0:T(8,128)(2,1)S(1)}, bf16[112,7168]{1,0:T(8,128)(2,1)S(1)}, f32[112,128]{1,0:T(8,128)S(1...) custom-call(bf16[224,3584]{1,0:T(8,128)(2,1)} %train_q.1, bf16[64,224]{1,0:T(8,128)(2,1)} %bitcast.12, ...), custom_call_target="tpu_custom_call" | custom-call | tf_op jit(solution)/shard_map/exchange/pallas_call | solution.py:372
  118.1 2.3 %finish.1 = (bf16[112,7168]{1,0:T(8,128)(2,1)}, bf16[112,7168]{1,0:T(8,128)(2,1)}, bf16[112,7168]{1,0:T(8,128)(2,1)}, f32[1,112]{1,0:T(1,128)}, f32[1,112]{1,0:T...) custom-call(bf16[112,7168]{1,0:T(8,128)(2,1)S(1)} %get-tuple-element.21.joined_q, ...), custom_call_target="tpu_custom_call" | custom-call | tf_op jit(solution)/shard_map/finish/pallas_call | solution.py:405
